TPU v7x, 512 devices: a whole 4x8x8 slice. The times are simulated.
512 devices in a mesh: roll: 64 (over z, y_lo, core), tensor: 8 (over x, y_hi).
Axes of the slice: x: 4, y: 8 (y_hi: 2, y_lo: 4; y = y_hi * 4 + y_lo), z: 8, core: 2. Of those that a mesh axis runs over, the one named last changes fastest.
Arguments:
- grad_out: bfloat16 [24576, 5120], P('roll', 'tensor'), may hold values from -6 to 6
- out_weight: bfloat16 [5120, 4096], P('roll', 'tensor'), may hold values from -0.078125 to 0.078125
- queries: bfloat16 [24576, 4096], P('roll', 'tensor'), may hold values from -6 to 6
- resp_key: bfloat16 [24576, 1024], P('roll', 'tensor'), may hold values from -5 to 5
- resp_value: bfloat16 [24576, 1024], P('roll', 'tensor'), may hold values from -5 to 5
- prefix_key: bfloat16 [256, 1024], P('roll', 'tensor'), may hold values from -5 to 5
- prefix_value: bfloat16 [256, 1024], P('roll', 'tensor'), may hold values from -5 to 5
- lengths: int32 [64], P('roll'), may hold values from 1 to 384
Outputs:
- grad_query: bfloat16 [24576, 4096], P('roll', 'tensor')
- grad_resp_key: bfloat16 [24576, 1024], P('roll', 'tensor')
- grad_resp_value: bfloat16 [24576, 1024], P('roll', 'tensor')
- grad_prefix_key: float32 [256, 1024], P('roll', 'tensor')
- grad_prefix_value: float32 [256, 1024], P('roll', 'tensor')
All inputs are finite; a program needn't handle non-finite values.
Results may differ from a plain program's by a relative error of at most 0.0063.
Values may be sent and summed in bfloat16 or wider, within the bound.
No kernel may reach another device: no remote copies, remote signals or barrier semaphores. Data moves between devices by JAX's collectives and lax.ppermute only.
A program may use at most 64 MiB of HBM per device.

v0:
```python
from functools import partial
import jax
import jax.numpy as jnp
from jax import lax
from jax.sharding import Mesh
from jax.sharding import PartitionSpec as P

HD = 128
ROWS = 384
ROLL = ("roll_0", "roll_1", "roll_2")


def in_order(parts, dim):
    parts = jnp.moveaxis(parts, 0, dim)
    shape = parts.shape
    return parts.reshape(*shape[:dim], shape[dim] * shape[dim + 1], *shape[dim + 2 :])


def stacked_from(x, axes, turns):
    parts = x[None]
    for k in turns:
        parts = lax.all_gather(parts, axes[k], axis=0, tiled=True)
    held = [lax.axis_size(axes[k]) for k in reversed(turns)]
    parts = parts.reshape(*held, *x.shape)
    turned = sorted(range(len(turns)), key=lambda place: turns[len(turns) - 1 - place])
    return parts.transpose(*turned, *range(len(turns), parts.ndim)).reshape(-1, *x.shape)


def gathered_by_axis(x, axes, turns, dim):
    return in_order(stacked_from(x, axes, turns), dim)


def side_by_side(arrays, axis, dim, along):
    widths = [a.shape[along] for a in arrays]
    both = jnp.concatenate(arrays, axis=along)
    whole = lax.all_gather(both, axis, axis=dim, tiled=True)
    return tuple(jnp.split(whole, [sum(widths[:k]) for k in range(1, len(widths))], axis=along))


def split_up(x, dim, length):
    before, after = (x.shape[:dim], x.shape[dim + 1 :])
    return jnp.moveaxis(x.reshape(*before, length, -1, *after), dim, 0)


def summed_on_arrival(x, axis, dim):
    length = lax.axis_size(axis)
    parts = lax.all_to_all(split_up(x, dim, length), axis, 0, 0, tiled=True)
    return jnp.sum(parts, axis=0)


def side_by_side_2(arrays, axis, dim, along):
    both = jnp.concatenate(arrays, axis=along)
    whole, at, done = (summed_on_arrival(both, axis, dim), 0, [])
    for a in arrays:
        done.append(lax.slice_in_dim(whole, at, at + a.shape[along], axis=along))
        at += a.shape[along]
    return tuple(done)


def block_terms(query_rows, grad_rows, offset, all_keys, all_values, prefix_rows, keep_prefix):
    row_count = query_rows.shape[0]
    local_heads = all_keys.shape[1] // HD
    group_size = query_rows.shape[1] // all_keys.shape[1]
    score_scale = HD ** (-0.5)
    query_heads = query_rows.reshape(row_count, local_heads, group_size, HD)
    grad_heads = grad_rows.reshape(row_count, local_heads, group_size, HD)
    key_heads = all_keys.reshape(-1, local_heads, HD)
    value_heads = all_values.reshape(-1, local_heads, HD)
    scores = (
        jnp.einsum("ikgd,jkd->kgij", query_heads, key_heads, preferred_element_type=jnp.float32)
        * score_scale
    )
    query_place = offset + jnp.arange(row_count, dtype=jnp.int32)[:, None]
    key_place = jnp.arange(key_heads.shape[0], dtype=jnp.int32)[None, :]
    allowed = (key_place < prefix_rows) | (key_place - prefix_rows <= query_place)
    scores = jnp.where(allowed, scores, -jnp.inf)
    row_max = jnp.max(scores, axis=-1, keepdims=True)
    shifted = jnp.exp(scores - row_max)
    row_total = jnp.sum(shifted, axis=-1, keepdims=True)
    soft_weights = shifted / row_total
    weights_low = soft_weights.astype(jnp.bfloat16)
    prob_grad = jnp.einsum(
        "ikgd,jkd->kgij", grad_heads, value_heads, preferred_element_type=jnp.float32
    )
    row_delta = jnp.sum(soft_weights * prob_grad, axis=-1, keepdims=True)
    score_low = (soft_weights * (prob_grad - row_delta) * score_scale).astype(jnp.bfloat16)
    query_grad = jnp.einsum(
        "kgij,jkd->ikgd", score_low, key_heads, preferred_element_type=jnp.float32
    )
    query_grad = query_grad.reshape(row_count, -1).astype(jnp.bfloat16)
    key_count = score_low.shape[-1]
    key_grad = jnp.einsum(
        "kgij,ikgd->jkd", score_low, query_heads, preferred_element_type=jnp.float32
    )
    value_grad = jnp.einsum(
        "kgij,ikgd->jkd", weights_low, grad_heads, preferred_element_type=jnp.float32
    )
    return (
        query_grad,
        key_grad.reshape(key_count, -1),
        value_grad.reshape(key_count, -1),
        row_max,
        row_total,
        row_delta,
    )


def body(grad_out, out_weight, queries, resp_key, resp_value, prefix_key, prefix_value, lengths):
    rows_here = queries.shape[0]
    responses = rows_here // ROWS
    full_grad = lax.all_gather(grad_out, "tensor", axis=1, tiled=True)
    projected = jnp.dot(
        full_grad,
        gathered_by_axis(out_weight, ROLL, (1, 0, 2), 0),
        preferred_element_type=jnp.float32,
    )
    position = jnp.arange(rows_here, dtype=jnp.int32)
    matches = (position // ROWS)[:, None] == jnp.arange(responses, dtype=jnp.int32)[None, :]
    row_limit = jnp.sum(jnp.where(matches, lengths[None, :], 0), axis=1)
    valid_rows = (position % ROWS < row_limit).astype(jnp.float32)
    out_grad = (projected * valid_rows[:, None]).astype(jnp.bfloat16)
    prefix_keys, prefix_values = side_by_side((prefix_key, prefix_value), ROLL, 0, 1)
    prefix_rows = prefix_keys.shape[0]
    key_width = prefix_key.shape[1]
    block_rows = min(128, ROWS)
    query_parts, key_parts, value_parts, saved = ([], [], [], [])
    all_keys = jnp.concatenate([prefix_keys, resp_key], axis=0)
    all_values = jnp.concatenate([prefix_values, resp_value], axis=0)
    key_rows = all_keys.shape[0]
    key_sum = jnp.zeros((key_rows, key_width), jnp.float32)
    value_sum = jnp.zeros((key_rows, key_width), jnp.float32)
    for part_index in range(ROWS // block_rows):
        offset = part_index * block_rows
        compute_block = partial(
            block_terms,
            queries[offset : offset + block_rows],
            out_grad[offset : offset + block_rows],
            offset,
            all_keys,
            all_values,
            prefix_rows,
            True,
        )
        result = compute_block()
        query_grad, key_grad, value_grad, row_max, row_total, row_delta = result
        query_parts.append(query_grad)
        key_sum = key_sum + key_grad
        value_sum = value_sum + value_grad
        saved.append((0, offset, offset, row_max, row_total, row_delta))
    prefix_key_sum = key_sum[:prefix_rows]
    prefix_value_sum = value_sum[:prefix_rows]
    key_sum = key_sum[prefix_rows:]
    value_sum = value_sum[prefix_rows:]
    key_parts.append(key_sum.astype(jnp.bfloat16))
    value_parts.append(value_sum.astype(jnp.bfloat16))
    grad_prefix_key, grad_prefix_value = side_by_side_2(
        (prefix_key_sum, prefix_value_sum), ROLL, 0, 1
    )
    grad_query = jnp.concatenate(query_parts, axis=0)
    grad_resp_key = key_parts[0]
    grad_resp_value = value_parts[0]
    return (grad_query, grad_resp_key, grad_resp_value, grad_prefix_key, grad_prefix_value)


def solution(mesh):
    torus = Mesh(
        mesh.devices.reshape(8, 4, 2, mesh.shape["tensor"]),
        ("roll_0", "roll_1", "roll_2", "tensor"),
    )
    placed = (
        P(ROLL, "tensor"),
        P(ROLL, "tensor"),
        P(ROLL, "tensor"),
        P(ROLL, "tensor"),
        P(ROLL, "tensor"),
        P(ROLL, "tensor"),
        P(ROLL, "tensor"),
        P(ROLL),
    )
    return jax.shard_map(
        body,
        mesh=torus,
        in_specs=placed,
        out_specs=(
            P(ROLL, "tensor"),
            P(ROLL, "tensor"),
            P(ROLL, "tensor"),
            P(ROLL, "tensor"),
            P(ROLL, "tensor"),
        ),
        check_vma=False,
    )
```

profile of v0, /device:TPU:1, one launch (start us, length us, event | category | flops | bytes accessed | tf_op | source)
XLA Modules:
  0.0 262.5 jit_solution(3908151491509216259)
XLA Ops:
  7.2 0.0 all-gather.8.cloned.1.call-start
  7.2 14.7 %all-gather = bf16[320,512]{1,0:T(8,128)(2,1)} all-gather(bf16[80,512]{1,0:T(8,128)(2,1)} %param.9), channel_id=2, replica_groups=mesh['roll_0'=8,'roll_1'=4,'roll_2'=2,'tensor'=8] {'roll_1'}, dimensions={0}, use_global_device_ids=true | all-gather | bytes 409600 | tf_op jit(solution)/shard_map/all_gather | solution.py:22
  21.9 0.0 all-gather.8.cloned.1.call-update
  21.9 0.0 all-gather.10.cloned.1.call-start
  21.9 48.3 %all-gather.8.cloned.1.call-done = bf16[32,80,512]{2,1,0:T(8,128)(2,1)} async-done(((bf16[4,80,512]{2,1,0:T(8,128)(2,1)}), bf16[32,80,512]{2,1,0:T(8,128)(2,1)}) %all-gather.8.cloned.1.call-update) | async-done | bytes 2621456 | tf_op jit(solution)/shard_map/all_gather | solution.py:22
  70.3 0.0 all-gather.10.cloned.1.call-update
  70.3 0.0 all-gather.6.cloned.1.call-start
  70.4 0.7 all-gather.6.cloned.1.call-update
  71.1 83.0 %all-gather.1 = bf16[64,4,256]{2,1,0:T(4,128)(2,1)S(1)} all-gather(bf16[1,4,256]{2,1,0:T(4,128)(2,1)S(1)} %maximum_bitcast_fusion.5), channel_id=1, replica_groups=mesh['roll_0'=8,'roll_1'=4,'roll_2'=2,'tensor'=8] {'roll_0','roll_1','ro..., dimensions={0}, use_global_device_ids=true | all-gather | bytes 133120 | tf_op jit(solution)/shard_map/all_gather | solution.py:36
  154.1 0.1 copy.150
  154.9 0.1 copy.151
  155.0 0.1 copy.149
  155.2 0.2 fusion.27
  155.5 0.3 fusion.44
  155.8 0.2 fusion.15
  156.0 0.3 fusion.43
  156.4 0.5 copy-done.2
  156.9 0.2 fusion.17
  157.1 0.3 fusion.45
  157.4 0.2 fusion.13
  157.6 0.0 all-gather.10.cloned.1.call-done
  157.6 5.3 %copy.102 = bf16[8,4,2,80,512]{4,3,2,1,0:T(8,128)(2,1)} copy(bf16[8,4,2,80,512]{4,3,1,0,2:T(8,128)(2,1)} %bitcast.153) | data formatting | bytes 10485760 | tf_op jit(solution)/shard_map/transpose | solution.py:26
  163.0 42.9 %all-gather.6.cloned.1.call-done = bf16[384,5120]{1,0:T(8,128)(2,1)} async-done(((bf16[384,640]{1,0:T(8,128)(2,1)}), bf16[384,5120]{1,0:T(8,128)(2,1)}) %all-gather.6.cloned.1.call-update) | async-done | bytes 3932176 | tf_op jit(solution)/shard_map/all_gather | solution.py:111
  205.9 5.9 %fusion.6 = bf16[384,512]{1,0:T(8,128)(2,1)S(1)} fusion(bf16[384,5120]{1,0:T(8,128)(2,1)} %all-gather.6.cloned.1.call-done, bf16[5120,512]{1,0:T(8,128)(2,1)} %bitcast.154, f32[384]{0:T(512)S(1)} %fusion.31), kind=kOutput, calls=%fused_computation.22 | convolution fusion | flops 2013659136 | bytes 9569792 | tf_op jit(solution)/shard_map/dot_general | solution.py:112
  211.7 0.7 fusion.40
  212.4 1.7 copy.153
  214.1 0.8 copy.154
  214.8 2.5 convolution_bitcast_fusion.4
  217.4 1.1 convolution_bitcast_fusion.3
  218.5 0.2 copy-done.3
  218.7 0.0 copy-done.10
  218.7 0.1 copy-done.13
  218.8 1.4 multiply_reduce_fusion.1
  220.2 1.4 multiply_reduce_fusion
  221.6 0.1 copy.152
  221.7 0.3 multiply_reduce_fusion.2
  222.1 0.6 copy-done.14
  222.7 0.1 copy-done.15
  222.8 0.4 fusion.11
  223.2 0.9 copy-done.4
  224.1 0.4 copy-done.6
  224.5 0.4 fusion.19
  224.9 0.3 convolution_bitcast_fusion.7
  225.2 0.6 copy-done.1
  225.8 0.4 copy-done.5
  226.2 0.4 fusion.20
  226.6 0.3 convolution_bitcast_fusion.6
  226.9 0.4 fusion.18
  227.3 0.3 fusion.8
  227.7 0.3 convolution_convert_fusion.2
  228.0 0.1 copy.128
  228.1 0.8 reshape.248
  228.9 12.9 %all-to-all-start = ((f32[64,4,256]{2,1,0:T(4,128)}), f32[64,4,256]{2,1,0:T(4,128)S(1)}, u32[]{:S(2)}, u32[]{:S(2)}) async-start(f32[64,4,256]{2,1,0:T(4,128)} %reshape.248), calls=%async_computation | async-start | bytes 524288 | tf_op jit(solution)/shard_map/all_to_all | solution.py:47
  241.8 0.8 copy.130
  242.6 0.8 copy.129
  243.3 0.1 copy.116
  243.5 0.3 convolution_convert_fusion.1
  243.8 0.1 copy.117
  243.9 0.3 convolution_convert_fusion
  244.2 0.1 copy.118
  244.3 0.8 pad_maximum_fusion
  245.1 10.3 %all-to-all-done = f32[64,4,256]{2,1,0:T(4,128)S(1)} async-done(((f32[64,4,256]{2,1,0:T(4,128)}), f32[64,4,256]{2,1,0:T(4,128)S(1)}, u32[]{:S(2)}, u32[]{:S(2)}) %all-to-all-start) | async-done | bytes 262176 | tf_op jit(solution)/shard_map/all_to_all | solution.py:47
  255.3 0.1 reduce_sum.73
  255.4 0.6 fusion.42
  (35 shorter events, 0.2 us)
Async XLA Ops:
  7.2 63.1 %all-gather.8.cloned.1.call-start = ((), (), s32[]{:S(2)}) async-start(), calls=%async_computation.2 | async-start | bytes 2949120 | tf_op jit(solution)/shard_map/all_gather | solution.py:22
  21.9 135.7 %all-gather.10.cloned.1.call-start = ((), (), s32[]{:S(2)}) async-start(), calls=%async_computation.3 | async-start | bytes 7864320 | tf_op jit(solution)/shard_map/all_gather | solution.py:22
  70.3 0.8 copy-start.11
  70.3 0.8 copy-start.12
  70.3 83.8 %copy-start.8 = (bf16[384,512]{1,0:T(8,128)(2,1)S(1)}, bf16[384,512]{1,0:T(8,128)(2,1)}, u32[]{:S(2)}) copy-start(bf16[384,512]{1,0:T(8,128)(2,1)} %param.10) | copy-start | bytes 1179652
  70.3 135.6 %all-gather.6.cloned.1.call-start = ((), (), s32[]{:S(2)}) async-start(), calls=%async_computation.1 | async-start | bytes 4423680 | tf_op jit(solution)/shard_map/all_gather | solution.py:111
  71.1 84.4 %copy-start.7 = (bf16[384,128]{1,0:T(8,128)(2,1)S(1)}, bf16[384,128]{1,0:T(8,128)(2,1)}, u32[]{:S(2)}) copy-start(bf16[384,128]{1,0:T(8,128)(2,1)} %param.11) | copy-start | bytes 294916
  155.8 1.1 copy-start.2
  156.9 63.3 %copy-start = (f32[1,4,128,640]{2,3,1,0:T(8,128)}, f32[1,4,128,640]{2,3,1,0:T(8,128)S(1)}, u32[]{:S(2)}) copy-start(f32[1,4,128,640]{2,3,1,0:T(8,128)S(1)} %get-tuple-element.39) | copy-start | bytes 3932164
  214.8 2.6 copy-start.9
  217.4 1.3 copy-start.3
  217.4 1.3 copy-start.10
  217.4 1.4 copy-start.13
  221.7 1.0 copy-start.14
  221.7 1.1 copy-start.15
  222.8 1.3 copy-start.4
  222.8 1.7 copy-start.6
  224.5 1.3 copy-start.1
  224.5 1.7 copy-start.5
  228.9 26.4 %all-to-all-start = ((f32[64,4,256]{2,1,0:T(4,128)}), f32[64,4,256]{2,1,0:T(4,128)S(1)}, u32[]{:S(2)}, u32[]{:S(2)}) async-start(f32[64,4,256]{2,1,0:T(4,128)} %reshape.248), calls=%async_computation | async-start | bytes 524288 | tf_op jit(solution)/shard_map/all_to_all | solution.py:47
Sparse Core Ops, SparseCore 0:
  22.0 48.2 all-gather.7
  72.4 26.1 all-gather.9
  101.7 104.0 all-gather.5
where the time goes:
time: 263 us
  waiting for transfers between devices  102 us (39%)
  blocking collectives  97.6 us (37%)
  local copies, waits for them, and re-layouts  16.2 us (6%)
  matrix products  16 us (6%)
  between operations  14.7 us (6%)
  starting transfers between devices  13 us (5%)
  other arithmetic  2.8 us (1%)
    all_gather x1, blocking collectives, side_by_side(): whole = lax.all_gather(both, axis, axis=dim, tiled=True)  83 us
    all_gather x2, waiting for transfers between devices, stacked_from(): parts = lax.all_gather(parts, axes[k], axis=0, tiled=True)  48.3 us
    all_gather x1, waiting for transfers between devices, body(): full_grad = lax.all_gather(grad_out, 'tensor', axis=1, tiled=True)  42.9 us
    all_gather x1, blocking collectives, stacked_from(): parts = lax.all_gather(parts, axes[k], axis=0, tiled=True)  14.7 us
    all_to_all x1, starting transfers between devices, summed_on_arrival(): parts = lax.all_to_all(split_up(x, dim, length), axis, 0, 0, tiled=True)  12.9 us
    all_to_all x1, waiting for transfers between devices, summed_on_arrival(): parts = lax.all_to_all(split_up(x, dim, length), axis, 0, 0, tiled=True)  10.3 us
    dot_general x1, matrix products, body(): jnp.dot(full_grad, gathered_by_axis(out_weight, ROLL, (1, 0, 2), 0), pref...  5.87 us
    unnamed x38, local copies, waits for them, and re-layouts  5.72 us
  transfers between devices with their start and end apart: 4, of which 3 were waited for; matrix products, arithmetic and copies ran while one was open for 4% of the time, Pallas kernels for 0%

commit v1 on v0

--- a/solution.py
+++ b/solution.py
@@ -19,7 +19,9 @@
 def stacked_from(x, axes, turns):
     parts = x[None]
     for k in turns:
-        parts = lax.all_gather(parts, axes[k], axis=0, tiled=True)
+        parts = jnp.concatenate(
+            lax.all_to_all(jnp.stack([parts] * lax.axis_size(axes[k])), axes[k], 0, 0), axis=0
+        )
     held = [lax.axis_size(axes[k]) for k in reversed(turns)]
     parts = parts.reshape(*held, *x.shape)
     turned = sorted(range(len(turns)), key=lambda place: turns[len(turns) - 1 - place])

time: 263 us -> 195 us (0.74)
  the two profiles are of different devices: /device:TPU:1 before, /device:TPU:58 now
where the time goes in v1:
time: 195 us; the launch traced here: 194 us
  blocking collectives  118 us (61%)
  starting transfers between devices  21.4 us (11%)
  local copies, waits for them, and re-layouts  15.6 us (8%)
  between operations  15.1 us (8%)
  matrix products  11.8 us (6%)
  waiting for transfers between devices  9.46 us (5%)
  other arithmetic  3.25 us (2%)
    all_gather x1, blocking collectives, side_by_side(): whole = lax.all_gather(both, axis, axis=dim, tiled=True)  96.2 us
    all_to_all x2, blocking collectives, stacked_from(): lax.all_to_all(jnp.stack([parts] * lax.axis_size(axes[k])), axes[k], 0, 0)  21.4 us
    all_to_all x1, starting transfers between devices, summed_on_arrival(): parts = lax.all_to_all(split_up(x, dim, length), axis, 0, 0, tiled=True)  10.9 us
    all_to_all x1, starting transfers between devices, stacked_from(): lax.all_to_all(jnp.stack([parts] * lax.axis_size(axes[k])), axes[k], 0, 0)  10.4 us
    all_to_all x1, waiting for transfers between devices, summed_on_arrival(): parts = lax.all_to_all(split_up(x, dim, length), axis, 0, 0, tiled=True)  8.78 us
    unnamed x26, local copies, waits for them, and re-layouts  7.09 us
    dot_general x1, matrix products, body(): jnp.dot(full_grad, gathered_by_axis(out_weight, ROLL, (1, 0, 2), 0), pref...  6.68 us
  transfers between devices with their start and end apart: 3, of which 1 were waited for; matrix products, arithmetic and copies ran while one was open for 6% of the time, Pallas kernels for 0%

profile of v1, /device:TPU:58, one launch (start us, length us, event | category | flops | bytes accessed | tf_op | source)
XLA Modules:
  0.0 194.3 jit_solution(10011941818483352851)
XLA Ops:
  7.2 0.0 all-gather.3.cloned.1.call-start
  7.2 0.7 all-gather.3.cloned.1.call-update
  7.9 0.9 stack.9
  8.8 13.5 %all_to_all.20 = bf16[4,1,80,512]{3,2,1,0:T(8,128)(2,1)S(1)} all-to-all(bf16[4,1,80,512]{3,2,1,0:T(8,128)(2,1)S(1)} %stack.9), channel_id=1, replica_groups=mesh['roll_0'=8,'roll_1'=4,'roll_2'=2,'tensor'=8] {'roll_1'}, dimensions={0} | all-to-all | bytes 655360 | tf_op jit(solution)/shard_map/all_to_all | solution.py:23
  22.3 1.8 stack.10
  24.1 10.4 %all-to-all-start.1 = ((bf16[8,4,80,512]{3,2,1,0:T(8,128)(2,1)}), bf16[8,4,80,512]{3,2,1,0:T(8,128)(2,1)S(1)}, u32[]{:S(2)}, u32[]{:S(2)}) async-start(bf16[8,4,80,512]{3,2,1,0:T(8,128)(2,1)} %stack.10), calls=%async_computation.1 | async-start | bytes 5242880 | tf_op jit(solution)/shard_map/all_to_all | solution.py:23
  34.6 0.0 copy-done.7
  34.6 0.0 copy-done.8
  34.6 0.0 copy-start.6
  34.6 96.2 %all-gather = bf16[64,4,256]{2,1,0:T(4,128)(2,1)S(1)} all-gather(bf16[1,4,256]{2,1,0:T(4,128)(2,1)S(1)} %maximum_bitcast_fusion.5), channel_id=1, replica_groups=mesh['roll_0'=8,'roll_1'=4,'roll_2'=2,'tensor'=8] {'roll_0','roll_1','ro..., dimensions={0}, use_global_device_ids=true | all-gather | bytes 133120 | tf_op jit(solution)/shard_map/all_gather | solution.py:38
  130.9 1.1 fusion.40
  131.9 0.1 copy.113
  132.7 0.1 copy.114
  132.8 0.1 copy.112
  133.0 0.2 fusion.28
  133.3 0.0 copy-done.6
  133.3 0.3 fusion.45
  133.6 0.0 copy-start.4
  133.6 0.2 fusion.16
  133.8 0.9 copy-done.4
  134.7 0.3 fusion.44
  135.0 0.0 copy-start.2
  135.0 0.2 fusion.18
  135.2 0.9 copy-done.2
  136.1 0.3 fusion.46
  136.4 1.1 copy-done
  137.5 0.2 fusion.14
  137.7 0.0 all-to-all-done.1
  137.7 0.5 pad_maximum_fusion
  138.2 7.9 %all_to_all.21 = bf16[2,32,80,512]{3,2,1,0:T(8,128)(2,1)S(1)} all-to-all(bf16[2,32,80,512]{3,2,1,0:T(8,128)(2,1)S(1)} %pad_maximum_fusion), channel_id=1, replica_groups=mesh['roll_0'=8,'roll_1'=4,'roll_2'=2,'tensor'=8] {'roll_2'}, dimensions={0} | all-to-all | bytes 10485760 | tf_op jit(solution)/shard_map/all_to_all | solution.py:23
  146.1 2.8 %copy.65 = bf16[2,32,80,512]{3,2,0,1:T(8,128)(2,1)} copy(bf16[2,32,80,512]{3,2,1,0:T(8,128)(2,1)S(1)} %all_to_all.21) | data formatting | bytes 10485760 | tf_op jit(solution)/shard_map/all_to_all | solution.py:23
  149.0 6.7 %fusion.7 = bf16[384,512]{0,1:T(8,128)(2,1)S(1)} fusion(bf16[5120,512]{1,0:T(8,128)(2,1)} %bitcast.158, bf16[384,5120]{1,0:T(8,128)(2,1)} %all-gather.3.cloned.1.call-done, f32[384]{0:T(512)S(1)} %fusion.32), kind=kOutput, calls=%fused_computation.24 | convolution fusion | flops 2013659136 | bytes 9569792 | tf_op jit(solution)/shard_map/dot_general | solution.py:114
  155.6 0.1 fusion.41
  155.7 0.4 convolution_bitcast_fusion.4
  156.1 0.9 copy-done.3
  157.1 0.4 convolution_bitcast_fusion.3
  157.4 0.5 copy-done.9
  157.9 0.4 multiply_reduce_fusion.1
  158.3 0.0 copy-start.1
  158.3 0.4 multiply_reduce_fusion
  158.7 0.9 copy-done.1
  159.6 0.4 multiply_reduce_fusion.2
  160.0 0.4 fusion.12
  160.4 0.4 fusion.20
  160.8 0.3 convolution_bitcast_fusion.7
  161.1 0.4 fusion.21
  161.5 0.3 convolution_bitcast_fusion.6
  161.8 0.4 fusion.19
  162.2 0.3 fusion.9
  162.6 0.3 convolution_convert_fusion.2
  162.9 0.1 copy.88
  163.1 0.8 reshape.248
  163.8 10.9 %all-to-all-start.3 = ((f32[64,4,256]{2,1,0:T(4,128)}), f32[64,4,256]{2,1,0:T(4,128)S(1)}, u32[]{:S(2)}, u32[]{:S(2)}) async-start(f32[64,4,256]{2,1,0:T(4,128)} %reshape.248), calls=%async_computation.3 | async-start | bytes 524288 | tf_op jit(solution)/shard_map/all_to_all | solution.py:49
  174.7 0.8 copy.90
  175.5 0.8 copy.89
  176.2 0.1 copy.79
  176.3 0.3 convolution_convert_fusion.1
  176.6 0.1 copy.80
  176.8 0.3 convolution_convert_fusion
  177.1 0.1 copy.81
  177.2 0.8 pad_maximum_fusion.1
  178.0 8.8 %all-to-all-done.3 = f32[64,4,256]{2,1,0:T(4,128)S(1)} async-done(((f32[64,4,256]{2,1,0:T(4,128)}), f32[64,4,256]{2,1,0:T(4,128)S(1)}, u32[]{:S(2)}, u32[]{:S(2)}) %all-to-all-start.3) | async-done | bytes 262176 | tf_op jit(solution)/shard_map/all_to_all | solution.py:49
  186.7 0.1 reduce_sum.73
  186.8 0.6 fusion.43
  (20 shorter events, 0.2 us)
Async XLA Ops:
  7.2 141.8 %all-gather.3.cloned.1.call-start = ((), (), s32[]{:S(2)}) async-start(), calls=%async_computation.4 | async-start | bytes 4423680 | tf_op jit(solution)/shard_map/all_gather | solution.py:113
  24.1 10.5 %copy-start.7 = (bf16[4,128]{1,0:T(4,128)(2,1)S(1)}, bf16[4,128]{1,0:T(4,128)(2,1)}, u32[]{:S(2)}) copy-start(bf16[4,128]{1,0:T(4,128)(2,1)} %param.14) | copy-start | bytes 3076
  24.1 10.5 %copy-start.8 = (bf16[4,128]{1,0:T(4,128)(2,1)S(1)}, bf16[4,128]{1,0:T(4,128)(2,1)}, u32[]{:S(2)}) copy-start(bf16[4,128]{1,0:T(4,128)(2,1)} %param.13) | copy-start | bytes 3076
  24.1 113.6 %all-to-all-start.1 = ((bf16[8,4,80,512]{3,2,1,0:T(8,128)(2,1)}), bf16[8,4,80,512]{3,2,1,0:T(8,128)(2,1)S(1)}, u32[]{:S(2)}, u32[]{:S(2)}) async-start(bf16[8,4,80,512]{3,2,1,0:T(8,128)(2,1)} %stack.10), calls=%async_computation.1 | async-start | bytes 5242880 | tf_op jit(solution)/shard_map/all_to_all | solution.py:23
  34.6 98.7 %copy-start.6 = (bf16[384,128]{1,0:T(8,128)(2,1)S(1)}, bf16[384,128]{1,0:T(8,128)(2,1)}, u32[]{:S(2)}) copy-start(bf16[384,128]{1,0:T(8,128)(2,1)} %param.11) | copy-start | bytes 294916
  133.6 1.1 copy-start.4
  135.0 1.1 copy-start.2
  136.4 1.1 copy-start
  149.0 6.8 %copy-start.5 = (f32[1,4,128,640]{2,3,1,0:T(8,128)S(1)}, f32[1,4,128,640]{2,3,1,0:T(8,128)}, u32[]{:S(2)}) copy-start(f32[1,4,128,640]{2,3,1,0:T(8,128)} %copy-done.4) | copy-start | bytes 3932164
  155.7 1.3 copy-start.3
  157.0 0.9 copy-start.9
  158.3 1.3 copy-start.1
  163.8 22.9 %all-to-all-start.3 = ((f32[64,4,256]{2,1,0:T(4,128)}), f32[64,4,256]{2,1,0:T(4,128)S(1)}, u32[]{:S(2)}, u32[]{:S(2)}) async-start(f32[64,4,256]{2,1,0:T(4,128)} %reshape.248), calls=%async_computation.3 | async-start | bytes 524288 | tf_op jit(solution)/shard_map/all_to_all | solution.py:49
Sparse Core Ops, SparseCore 0:
  11.2 102.4 all-gather.2
